TPU v7x, 256 devices: a whole 4x4x8 slice. The times are simulated.
256 devices in a mesh: mem: 32 (over x, z_lo, y), tile: 8 (over z_hi, core).
Axes of the slice: x: 4, y: 4, z: 8 (z_hi: 4, z_lo: 2; z = z_hi * 2 + z_lo), core: 2. Of those that a mesh axis runs over, the one named last changes fastest.
Arguments:
- starting_samples: float32 [512, 512, 512], P('mem', 'tile'), may hold values from -6 to 6
- transport_number_vertical: float32 [512, 512], P('tile'), may hold values from 0.1 to 0.35
- transport_number_horizontal: float32 [512, 512], P('tile'), may hold values from 0.1 to 0.35
- spreading_number: float32 [512, 512], P('tile'), may hold values from 0.01 to 0.07
- obs_value: float32 [8, 32, 128], P('tile'), may hold values from -6 to 6
- obs_error: float32 [8, 32, 128], P('tile'), may hold values from 0.002 to 0.05
- obs_index: int32 [8, 32, 128], P('tile'), may hold values from 0 to 1023
- loc_index: int32 [8, 32, 128], P('tile'), may hold values from 0 to 7
- loc_table: float32 [3, 8], replicated, may hold values from 0.2 to 1
Outputs:
- analysis: float32 [512, 512, 512], P('mem', 'tile')
Inputs may be any that keep to these rules, and one draw needn't show every extreme that they name: Observation j of a patch lies in the patch's cell obs_index, cells numbered row by row, 16 to a row.
All inputs are finite; a program needn't handle non-finite values.
Results may differ from a plain program's by a relative error of at most 0.0003.
Values sent between devices are 32-bit elements; how exact they have to be, the bound alone decides.
A program may use at most 128 MiB of HBM per device.

v0:
```python
import functools

import jax
import jax.numpy as jnp
from jax import lax
from jax.experimental import pallas as pl
from jax.experimental.pallas import tpu as pltpu
from jax.sharding import PartitionSpec as P

PASSES = 6
NS_ITERS = 8
PAD = 8
ROWS = 64
COLS = 16
MESH = pl.DeviceIdType.MESH
VMEM_LIMIT = 62 * 1024 * 1024


def split(x):
    high = x.astype(jnp.bfloat16)
    low = (x - high.astype(jnp.float32)).astype(jnp.bfloat16)
    return high, low


def dot(a, b):
    return jnp.dot(a, b, preferred_element_type=jnp.float32)


def dot3(a_high, a_low, b_high, b_low):
    return dot(a_high, b_high) + (dot(a_high, b_low) + dot(a_low, b_high))


def exchange_groups(rows, group):
    rows = list(rows)
    for bit in range(3):
        step = 1 << bit
        keep = (group & step) == 0
        for i in range(8):
            if i & step:
                continue
            a, b = rows[i], rows[i + step]
            rows[i] = jnp.where(keep, a, pltpu.roll(b, COLS * step, 1))
            rows[i + step] = jnp.where(keep, pltpu.roll(a, 128 - COLS * step, 1), b)
    return rows


def main_kernel(
    field,
    coef_x,
    coef_y,
    coef_mix,
    obs_value,
    obs_error,
    obs_index,
    loc_index,
    loc_table,
    back,
    levels,
    raw,
    coef,
    packed,
    picked,
    members,
    seen,
    matrix,
    root,
    matrix_parts,
    root_parts,
    factor_parts,
    anomaly_parts,
    result,
    load_sem,
    halo_send,
    halo_recv,
    seen_send,
    seen_recv,
    patch_send,
    patch_recv,
    back_send,
    back_recv,
    *,
    parts,
    tiles,
):
    me = lax.axis_index("mem")
    tile = lax.axis_index("tile")
    own = field.shape[0]
    width = field.shape[2]
    size = own * parts
    cells = ROWS * COLS
    nobs = obs_value.shape[2]
    lane_tiles = width // 128
    below = lax.rem(tile + 1, tiles)
    above = lax.rem(tile + tiles - 1, tiles)

    def peer(k):
        return lax.rem(me + 11 * k, parts)

    def source(k):
        return lax.rem(me + 12 * parts - 11 * k, parts)

    loads = []
    for m in range(own):
        loads.append(
            pltpu.make_async_copy(
                field.at[m], levels.at[0, pl.ds(PAD, ROWS), m], load_sem.at[m]
            )
        )
    for i, ref in enumerate((coef_x, coef_y, coef_mix)):
        loads.append(
            pltpu.make_async_copy(ref, raw.at[i, pl.ds(PAD, ROWS)], load_sem.at[own + i])
        )
    for load in loads:
        load.start()

    barrier = pltpu.get_barrier_semaphore()

    def greet(k, carry):
        pl.semaphore_signal(barrier, inc=1, device_id=(peer(k), tile), device_id_type=MESH)
        return carry

    pl.semaphore_signal(barrier, inc=1, device_id=(me, below), device_id_type=MESH)
    pl.semaphore_signal(barrier, inc=1, device_id=(me, above), device_id_type=MESH)
    lax.fori_loop(1, parts, greet, 0)
    pl.semaphore_wait(barrier, parts + 1)
    for load in loads:
        load.wait()

    halo = []
    for number, (target, src, dst) in enumerate(
        (
            (below, PAD + ROWS - PASSES, PAD - PASSES),
            (above, PAD, PAD + ROWS),
        )
    ):
        halo.append(
            pltpu.make_async_remote_copy(
                src_ref=levels.at[0, pl.ds(src, PASSES)],
                dst_ref=levels.at[0, pl.ds(dst, PASSES)],
                send_sem=halo_send.at[number],
                recv_sem=halo_recv.at[number],
                device_id=(me, target),
                device_id_type=MESH,
            )
        )
    for number, (target, src, dst) in enumerate(
        ((below, ROWS, 0), (above, PAD, PAD + ROWS))
    ):
        halo.append(
            pltpu.make_async_remote_copy(
                src_ref=raw.at[:, pl.ds(src, PAD)],
                dst_ref=raw.at[:, pl.ds(dst, PAD)],
                send_sem=halo_send.at[2 + number],
                recv_sem=halo_recv.at[2 + number],
                device_id=(me, target),
                device_id_type=MESH,
            )
        )
    for copy in halo:
        copy.start()

    def widen(row, carry):
        sx = raw[0, pl.ds(row, 1), :]
        sy = raw[1, pl.ds(row, 1), :]
        mix = raw[2, pl.ds(row, 1), :]
        for i, value in enumerate((1.0 - sx - sy - 4.0 * mix, sx + mix, sy + mix, mix)):
            coef[i, row] = jnp.broadcast_to(value, (8, width))
        return carry

    def step(level, first, count):
        def one(i, carry):
            row = first + i
            for half in range(own // 8):
                at = pl.ds(8 * half, 8)
                middle = levels[level, row, at, :]
                north = levels[level, row - 1, at, :]
                south = levels[level, row + 1, at, :]
                west = pltpu.roll(middle, 1, 1)
                east = pltpu.roll(middle, width - 1, 1)
                levels[level + 1, row, at, :] = (
                    coef[0, row] * middle + coef[1, row] * west
                ) + (coef[2, row] * north + coef[3, row] * (south + east))
            return carry

        lax.fori_loop(0, count, one, 0, unroll=2)

    lax.fori_loop(PAD, PAD + ROWS, widen, 0)
    for k in range(1, PASSES):
        step(k - 1, PAD + k, ROWS - 2 * k)
    for copy in halo:
        copy.wait_recv()
    lax.fori_loop(PAD - PASSES, PAD, widen, 0)
    lax.fori_loop(PAD + ROWS, PAD + ROWS + PASSES, widen, 0)
    for k in range(1, PASSES):
        step(k - 1, PAD - PASSES + k, PASSES)
        step(k - 1, PAD + ROWS - k, PASSES)
    step(PASSES - 1, PAD, ROWS)

    group = lax.broadcasted_iota(jnp.int32, (8, 128), 1) // COLS

    def pack(g, carry):
        lanes = pl.ds(pl.multiple_of(g * 128, 128), 128)
        for half in range(own // 8):
            at = pl.ds(8 * half, 8)
            for block in range(lane_tiles):
                rows = [
                    levels[PASSES, PAD + 8 * g + r, at, pl.ds(128 * block, 128)]
                    for r in range(8)
                ]
                for p, value in enumerate(exchange_groups(rows, group)):
                    packed[8 * block + p, at, lanes] = value
        return carry

    lax.fori_loop(0, ROWS // 8, pack, 0)

    def pick(b, carry):
        index = jnp.broadcast_to(obs_index[0, pl.ds(b, 1), :], (8, nobs))
        lane = index % 128
        place = index // 128
        for half in range(own // 8):
            at = pl.ds(8 * half, 8)
            total = jnp.zeros((8, nobs), jnp.float32)
            for g in range(cells // 128):
                found = jnp.take_along_axis(
                    packed[b, at, pl.ds(128 * g, 128)], lane, axis=1, mode="promise_in_bounds"
                )
                total = jnp.where(place == g, found, total)
            picked[b + 1, at, :] = total
        return carry

    lax.fori_loop(0, parts, pick, 0)
    picked[0] = picked[parts]
    picked[parts + 1] = picked[1]

    mine = pl.ds(pl.multiple_of(own * me, own), own)

    def seen_copy(k):
        return pltpu.make_async_remote_copy(
            src_ref=picked.at[pl.ds(peer(k), 3)],
            dst_ref=seen.at[:, mine],
            send_sem=seen_send.at[k],
            recv_sem=seen_recv.at[me],
            device_id=(peer(k), tile),
            device_id_type=MESH,
        )

    def patch_copy(k):
        return pltpu.make_async_remote_copy(
            src_ref=packed.at[peer(k)],
            dst_ref=members.at[mine],
            send_sem=patch_send.at[k],
            recv_sem=patch_recv.at[me],
            device_id=(peer(k), tile),
            device_id_type=MESH,
        )

    def back_copy(k):
        rows = pl.ds(pl.multiple_of(own * peer(k), own), own)
        return pltpu.make_async_remote_copy(
            src_ref=result.at[rows],
            dst_ref=back.at[me],
            send_sem=back_send.at[k],
            recv_sem=back_recv.at[me],
            device_id=(peer(k), tile),
            device_id_type=MESH,
        )

    def start_all(make):
        def one(k, carry):
            make(k).start()
            return carry

        lax.fori_loop(1, parts, one, 0)

    def wait_send_all(make):
        def one(k, carry):
            make(k).wait_send()
            return carry

        lax.fori_loop(1, parts, one, 0)

    def wait_seen(k, carry):
        rows = pl.ds(pl.multiple_of(own * source(k), own), own)
        pltpu.make_async_remote_copy(
            src_ref=picked.at[pl.ds(0, 3)],
            dst_ref=seen.at[:, rows],
            send_sem=seen_send.at[k],
            recv_sem=seen_recv.at[source(k)],
            device_id=(peer(k), tile),
            device_id_type=MESH,
        ).wait_recv()
        return carry

    def wait_patch(k, carry):
        rows = pl.ds(pl.multiple_of(own * source(k), own), own)
        pltpu.make_async_remote_copy(
            src_ref=packed.at[0],
            dst_ref=members.at[rows],
            send_sem=patch_send.at[k],
            recv_sem=patch_recv.at[source(k)],
            device_id=(peer(k), tile),
            device_id_type=MESH,
        ).wait_recv()
        return carry

    def wait_back(k, carry):
        pltpu.make_async_remote_copy(
            src_ref=result.at[pl.ds(0, own)],
            dst_ref=back.at[source(k)],
            send_sem=back_send.at[k],
            recv_sem=back_recv.at[source(k)],
            device_id=(peer(k), tile),
            device_id_type=MESH,
        ).wait_recv()
        return carry

    start_all(seen_copy)
    start_all(patch_copy)
    for role in range(3):
        seen[role, mine, :] = picked[me + role]
    members[mine, :] = packed[me]
    lax.fori_loop(1, parts, wait_seen, 0)

    row_id = lax.broadcasted_iota(jnp.int32, (size, size), 0)
    column_id = lax.broadcasted_iota(jnp.int32, (size, size), 1)
    diagonal = row_id == column_id
    gram = jnp.where(diagonal, size - 1.0, 0.0)
    pull = jnp.zeros((size, 1), jnp.float32)
    for role in range(3):
        patch = lax.rem(me + role + parts - 1, parts)
        value = obs_value[0, pl.ds(patch, 1), :]
        error = obs_error[0, pl.ds(patch, 1), :]
        level = loc_index[0, pl.ds(patch, 1), :]
        weight = jnp.zeros_like(value)
        for i in range(loc_table.shape[1]):
            weight = weight + jnp.where(level == i, loc_table[role, i], 0.0)
        precision = weight / error
        observed = seen[role]
        obs_mean = jnp.sum(observed, axis=0, keepdims=True) * (1.0 / size)
        spread = observed - obs_mean
        pull = pull + jnp.sum(
            spread * (precision * (value - obs_mean)), axis=1, keepdims=True
        )
        left_high, left_low = split(spread * precision)
        right_high, right_low = split(spread)
        gram = gram + sum(
            lax.dot_general(
                a, b, (((1,), (1,)), ((), ())), preferred_element_type=jnp.float32
            )
            for a, b in (
                (left_high, right_high),
                (left_high, right_low),
                (left_low, right_high),
                (left_low, right_low),
            )
        )
    square = jnp.sum(jnp.sum(gram * gram, axis=0, keepdims=True), axis=1, keepdims=True)
    inverse_scale = lax.rsqrt(square)
    inverse_scale = 1.0 / jnp.sqrt(square)

    def put(parts_ref, value):
        high, low = split(value)
        parts_ref[0] = high
        parts_ref[1] = low

    def product(a, b):
        return dot3(a[0], a[1], b[0], b[1])

    scaled = gram * inverse_scale
    put(matrix_parts, scaled)
    factor = jnp.where(diagonal, 1.5, 0.0) - 0.5 * scaled
    put(factor_parts, factor)
    put(root_parts, factor)
    put(matrix_parts, product(matrix_parts, factor_parts))

    def iterate(i, carry):
        put(
            factor_parts,
            jnp.where(diagonal, 1.5, 0.0) - 0.5 * product(root_parts, matrix_parts),
        )
        put(matrix_parts, product(matrix_parts, factor_parts))
        put(root_parts, product(factor_parts, root_parts))
        return carry

    lax.fori_loop(0, NS_ITERS - 2, iterate, 0)
    put(
        factor_parts,
        jnp.where(diagonal, 1.5, 0.0) - 0.5 * product(root_parts, matrix_parts),
    )
    root[...] = product(factor_parts, root_parts)

    pull_row = jnp.sum(jnp.where(diagonal, pull, 0.0), axis=0, keepdims=True)
    once = jnp.sum(root[...] * pull_row, axis=1, keepdims=True)
    mean_weight = jnp.sum(root[...] * once, axis=0, keepdims=True) * inverse_scale
    put(root_parts, jnp.sqrt((size - 1.0) * inverse_scale) * root[...] + mean_weight)

    lax.fori_loop(1, parts, wait_patch, 0)
    chunk = 256
    for c in range(cells // chunk):
        lanes = pl.ds(chunk * c, chunk)
        block = members[:, lanes]
        center = jnp.sum(block, axis=0, keepdims=True) * (1.0 / size)
        high, low = split(block - center)
        result[:, lanes] = center + dot3(root_parts[0], root_parts[1], high, low)
    start_all(back_copy)
    back[me] = result[mine, :]
    lax.fori_loop(1, parts, wait_back, 0)
    for copy in halo:
        copy.wait_send()
    wait_send_all(seen_copy)
    wait_send_all(patch_copy)
    wait_send_all(back_copy)


def unpack_kernel(back, out, rows_ref, sem):
    own = back.shape[1]
    lane_tiles = rows_ref.shape[2] // 128
    group = lax.broadcasted_iota(jnp.int32, (8, 128), 1) // COLS

    def unpack(g, carry):
        lanes = pl.ds(pl.multiple_of(g * 128, 128), 128)
        for half in range(own // 8):
            at = pl.ds(8 * half, 8)
            for block in range(lane_tiles):
                values = [back[8 * block + p, at, lanes] for p in range(8)]
                for r, value in enumerate(exchange_groups(values, group)):
                    rows_ref[8 * g + r, at, pl.ds(128 * block, 128)] = value
        return carry

    lax.fori_loop(0, ROWS // 8, unpack, 0)
    copies = [
        pltpu.make_async_copy(rows_ref.at[:, m], out.at[m], sem.at[m]) for m in range(own)
    ]
    for copy in copies:
        copy.start()
    for copy in copies:
        copy.wait()


def body(*args, parts, tiles):
    field = args[0]
    own, _, width = field.shape
    size = own * parts
    cells = ROWS * COLS
    nobs = args[4].shape[2]
    f32 = jnp.float32
    dma = pltpu.SemaphoreType.DMA
    hbm = pl.BlockSpec(memory_space=pl.ANY)
    vmem = pl.BlockSpec(memory_space=pltpu.VMEM)
    smem = pl.BlockSpec(memory_space=pltpu.SMEM)
    tall = ROWS + 2 * PAD
    pair = pltpu.VMEM((2, size, size), jnp.bfloat16)
    back = pl.pallas_call(
        functools.partial(main_kernel, parts=parts, tiles=tiles),
        out_shape=jax.ShapeDtypeStruct((parts, own, cells), f32),
        in_specs=[hbm] * 4 + [vmem] * 4 + [smem],
        out_specs=vmem,
        scratch_shapes=[
            pltpu.VMEM((PASSES + 1, tall, own, width), f32),
            pltpu.VMEM((3, tall, width), f32),
            pltpu.VMEM((4, tall, 8, width), f32),
            pltpu.VMEM((parts, own, cells), f32),
            pltpu.VMEM((parts + 2, own, nobs), f32),
            pltpu.VMEM((size, cells), f32),
            pltpu.VMEM((3, size, nobs), f32),
            pltpu.VMEM((8, 128), f32),
            pltpu.VMEM((size, size), f32),
            pair,
            pair,
            pair,
            pltpu.VMEM((8, 128), f32),
            pltpu.VMEM((size, cells), f32),
            dma((own + 3,)),
            dma((4,)),
            dma((4,)),
            dma((parts,)),
            dma((parts,)),
            dma((parts,)),
            dma((parts,)),
            dma((parts,)),
            dma((parts,)),
        ],
        compiler_params=pltpu.CompilerParams(
            collective_id=0, has_side_effects=True, vmem_limit_bytes=VMEM_LIMIT
        ),
        name="forecast_and_analysis",
    )(*args)
    return pl.pallas_call(
        unpack_kernel,
        out_shape=jax.ShapeDtypeStruct(field.shape, f32),
        in_specs=[vmem],
        out_specs=hbm,
        scratch_shapes=[pltpu.VMEM((ROWS, own, width), f32), dma((own,))],
        name="unpack",
    )(back)


def solution(mesh):
    parts, tiles = mesh.shape["mem"], mesh.shape["tile"]
    in_specs = (
        P("mem", "tile", None),
        P("tile", None),
        P("tile", None),
        P("tile", None),
        P("tile", None, None),
        P("tile", None, None),
        P("tile", None, None),
        P("tile", None, None),
        P(),
    )
    return jax.shard_map(
        functools.partial(body, parts=parts, tiles=tiles),
        mesh=mesh,
        in_specs=in_specs,
        out_specs=P("mem", "tile", None),
        check_vma=False,
    )
```

profile of v0, /device:TPU:1, one launch (start us, length us, event | category | flops | bytes accessed | tf_op | source)
XLA Modules:
  0.0 122.9 jit_solution(11022322793740105833)
XLA Ops:
  0.0 116.9 %forecast_and_analysis.1.back = f32[32,16,1024]{2,1,0:T(8,128)} custom-call(f32[16,64,512]{2,1,0:T(8,128)} %field.1, f32[64,512]{1,0:T(8,128)} %coef_x.1, f32[64,512]{1,0:T(8,128)} %coef_y.1, f32[64,512]{1,0:T(8,128)} %coef_mix.1, f32[1,32,128]{2,1,0:T(8,128)} %obs_value.1, f32[1,32,128]{2,1,0:T(8,128)} %obs_error.1, s32[1,32,128]{2,1,0:T(8,128)} %obs_index.1, ...), custom_call_target="tpu_custom_call" | custom-call | tf_op jit(solution)/shard_map/forecast_and_analysis/pallas_call | solution.py:453
  116.9 6.0 %unpack.1 = f32[16,64,512]{2,1,0:T(8,128)} custom-call(f32[32,16,1024]{2,1,0:T(8,128)} %forecast_and_analysis.1.back), custom_call_target="tpu_custom_call" | custom-call | tf_op jit(solution)/shard_map/unpack/pallas_call | solution.py:488
where the time goes:
time: 123 us
  Pallas kernels  123 us (100%)
    pallas_call x1, Pallas kernels, body(): pl.pallas_call(functools.partial(main_kernel, parts=parts, tiles=tiles),...  117 us
    pallas_call x1, Pallas kernels, body(): pl.pallas_call(unpack_kernel, out_shape=jax.ShapeDtypeStruct(field.shape,...  6.01 us

commit v1 on v0

--- a/solution.py
+++ b/solution.py
@@ -12,6 +12,8 @@
 PAD = 8
 ROWS = 64
 COLS = 16
+UNROLL = 8
+CHUNKS = 2
 MESH = pl.DeviceIdType.MESH
 VMEM_LIMIT = 62 * 1024 * 1024
 
@@ -54,7 +56,7 @@
     obs_index,
     loc_index,
     loc_table,
-    back,
+    out,
     levels,
     raw,
     coef,
@@ -62,14 +64,15 @@
     picked,
     members,
     seen,
-    matrix,
     root,
     matrix_parts,
     root_parts,
     factor_parts,
-    anomaly_parts,
+    back,
     result,
     load_sem,
+    out_sem,
+    news_sem,
     halo_send,
     halo_recv,
     seen_send,
@@ -113,16 +116,33 @@
     for load in loads:
         load.start()
 
+    x, z, y = me // 8, (me // 4) % 2, me % 4
+    x_size = parts // 8
+    x_near = [lax.rem(x + i, x_size) * 8 + z * 4 + y for i in (1, x_size - 1)]
+    z_near = [x * 8 + (1 - z) * 4 + y]
+    y_near = [x * 8 + z * 4 + lax.rem(y + i, 4) for i in (1, 3)]
+    if x_size == 1:
+        x_near = []
+
+    def signal(semaphore, peers):
+        for one in peers:
+            pl.semaphore_signal(
+                semaphore, inc=1, device_id=(one, tile), device_id_type=MESH
+            )
+
     barrier = pltpu.get_barrier_semaphore()
-
-    def greet(k, carry):
-        pl.semaphore_signal(barrier, inc=1, device_id=(peer(k), tile), device_id_type=MESH)
-        return carry
-
     pl.semaphore_signal(barrier, inc=1, device_id=(me, below), device_id_type=MESH)
     pl.semaphore_signal(barrier, inc=1, device_id=(me, above), device_id_type=MESH)
-    lax.fori_loop(1, parts, greet, 0)
-    pl.semaphore_wait(barrier, parts + 1)
+    signal(barrier, y_near + z_near + x_near)
+    pl.semaphore_wait(barrier, 2 + len(y_near + z_near + x_near))
+
+    def spread_news():
+        for number, peers in enumerate((y_near, x_near, x_near, z_near)):
+            if peers:
+                signal(news_sem.at[number], peers)
+                yield
+                pl.semaphore_wait(news_sem.at[number], len(peers))
+
     for load in loads:
         load.wait()
 
@@ -167,34 +187,28 @@
             coef[i, row] = jnp.broadcast_to(value, (8, width))
         return carry
 
+    def advance(level, row):
+        for half in range(own // 8):
+            at = pl.ds(8 * half, 8)
+            middle = levels[level, row, at, :]
+            north = levels[level, row - 1, at, :]
+            south = levels[level, row + 1, at, :]
+            west = pltpu.roll(middle, 1, 1)
+            east = pltpu.roll(middle, width - 1, 1)
+            levels[level + 1, row, at, :] = (
+                coef[0, row] * middle + coef[1, row] * west
+            ) + (coef[2, row] * north + coef[3, row] * (south + east))
+
     def step(level, first, count):
-        def one(i, carry):
-            row = first + i
-            for half in range(own // 8):
-                at = pl.ds(8 * half, 8)
-                middle = levels[level, row, at, :]
-                north = levels[level, row - 1, at, :]
-                south = levels[level, row + 1, at, :]
-                west = pltpu.roll(middle, 1, 1)
-                east = pltpu.roll(middle, width - 1, 1)
-                levels[level + 1, row, at, :] = (
-                    coef[0, row] * middle + coef[1, row] * west
-                ) + (coef[2, row] * north + coef[3, row] * (south + east))
+        def several(i, carry):
+            for j in range(UNROLL):
+                advance(level, first + UNROLL * i + j)
             return carry
 
-        lax.fori_loop(0, count, one, 0, unroll=2)
-
-    lax.fori_loop(PAD, PAD + ROWS, widen, 0)
-    for k in range(1, PASSES):
-        step(k - 1, PAD + k, ROWS - 2 * k)
-    for copy in halo:
-        copy.wait_recv()
-    lax.fori_loop(PAD - PASSES, PAD, widen, 0)
-    lax.fori_loop(PAD + ROWS, PAD + ROWS + PASSES, widen, 0)
-    for k in range(1, PASSES):
-        step(k - 1, PAD - PASSES + k, PASSES)
-        step(k - 1, PAD + ROWS - k, PASSES)
-    step(PASSES - 1, PAD, ROWS)
+        trips = count // UNROLL
+        lax.fori_loop(0, trips, several, 0)
+        for row in range(first + UNROLL * trips, first + count):
+            advance(level, row)
 
     group = lax.broadcasted_iota(jnp.int32, (8, 128), 1) // COLS
 
@@ -211,7 +225,24 @@
                     packed[8 * block + p, at, lanes] = value
         return carry
 
-    lax.fori_loop(0, ROWS // 8, pack, 0)
+    lax.fori_loop(PAD, PAD + ROWS, widen, 0, unroll=4)
+    news = spread_news()
+    for k in range(1, PASSES + 1):
+        step(k - 1, PAD + k, ROWS - 2 * k)
+        next(news, None)
+    lax.fori_loop(1, ROWS // 8 - 1, pack, 0)
+    for copy in halo:
+        copy.wait_recv()
+    lax.fori_loop(PAD - PASSES, PAD, widen, 0, unroll=6)
+    lax.fori_loop(PAD + ROWS, PAD + ROWS + PASSES, widen, 0, unroll=6)
+    for k in range(1, PASSES + 1):
+        for i in range(PASSES):
+            advance(k - 1, PAD - PASSES + k + i)
+            advance(k - 1, PAD + ROWS - k + i)
+    pack(0, 0)
+    pack(ROWS // 8 - 1, 0)
+    for _ in news:
+        pass
 
     def pick(b, carry):
         index = jnp.broadcast_to(obs_index[0, pl.ds(b, 1), :], (8, nobs))
@@ -228,7 +259,7 @@
             picked[b + 1, at, :] = total
         return carry
 
-    lax.fori_loop(0, parts, pick, 0)
+    lax.fori_loop(0, parts, pick, 0, unroll=4)
     picked[0] = picked[parts]
     picked[parts + 1] = picked[1]
 
@@ -244,82 +275,99 @@
             device_id_type=MESH,
         )
 
-    def patch_copy(k):
+    piece = cells // CHUNKS
+
+    def patch_copy(c):
+        lanes = pl.ds(piece * c, piece)
+
+        def one(k):
+            return pltpu.make_async_remote_copy(
+                src_ref=packed.at[peer(k), :, lanes],
+                dst_ref=members.at[mine, lanes],
+                send_sem=patch_send.at[c, k],
+                recv_sem=patch_recv.at[c, me],
+                device_id=(peer(k), tile),
+                device_id_type=MESH,
+            )
+
+        return one
+
+    def back_copy(c):
+        lanes = pl.ds(piece * c, piece)
+
+        def one(k):
+            rows = pl.ds(pl.multiple_of(own * peer(k), own), own)
+            return pltpu.make_async_remote_copy(
+                src_ref=result.at[rows, lanes],
+                dst_ref=back.at[me, :, lanes],
+                send_sem=back_send.at[c, k],
+                recv_sem=back_recv.at[c, me],
+                device_id=(peer(k), tile),
+                device_id_type=MESH,
+            )
+
+        return one
+
+    def seen_arrival(k):
+        rows = pl.ds(pl.multiple_of(own * source(k), own), own)
         return pltpu.make_async_remote_copy(
-            src_ref=packed.at[peer(k)],
-            dst_ref=members.at[mine],
-            send_sem=patch_send.at[k],
-            recv_sem=patch_recv.at[me],
-            device_id=(peer(k), tile),
-            device_id_type=MESH,
-        )
-
-    def back_copy(k):
-        rows = pl.ds(pl.multiple_of(own * peer(k), own), own)
-        return pltpu.make_async_remote_copy(
-            src_ref=result.at[rows],
-            dst_ref=back.at[me],
-            send_sem=back_send.at[k],
-            recv_sem=back_recv.at[me],
-            device_id=(peer(k), tile),
-            device_id_type=MESH,
-        )
-
-    def start_all(make):
-        def one(k, carry):
-            make(k).start()
-            return carry
-
-        lax.fori_loop(1, parts, one, 0)
-
-    def wait_send_all(make):
-        def one(k, carry):
-            make(k).wait_send()
-            return carry
-
-        lax.fori_loop(1, parts, one, 0)
-
-    def wait_seen(k, carry):
-        rows = pl.ds(pl.multiple_of(own * source(k), own), own)
-        pltpu.make_async_remote_copy(
             src_ref=picked.at[pl.ds(0, 3)],
             dst_ref=seen.at[:, rows],
             send_sem=seen_send.at[k],
             recv_sem=seen_recv.at[source(k)],
             device_id=(peer(k), tile),
             device_id_type=MESH,
-        ).wait_recv()
-        return carry
-
-    def wait_patch(k, carry):
-        rows = pl.ds(pl.multiple_of(own * source(k), own), own)
-        pltpu.make_async_remote_copy(
-            src_ref=packed.at[0],
-            dst_ref=members.at[rows],
-            send_sem=patch_send.at[k],
-            recv_sem=patch_recv.at[source(k)],
-            device_id=(peer(k), tile),
-            device_id_type=MESH,
-        ).wait_recv()
-        return carry
-
-    def wait_back(k, carry):
-        pltpu.make_async_remote_copy(
-            src_ref=result.at[pl.ds(0, own)],
-            dst_ref=back.at[source(k)],
-            send_sem=back_send.at[k],
-            recv_sem=back_recv.at[source(k)],
-            device_id=(peer(k), tile),
-            device_id_type=MESH,
-        ).wait_recv()
-        return carry
-
-    start_all(seen_copy)
-    start_all(patch_copy)
+        )
+
+    def patch_arrival(c):
+        lanes = pl.ds(piece * c, piece)
+
+        def one(k):
+            rows = pl.ds(pl.multiple_of(own * source(k), own), own)
+            return pltpu.make_async_remote_copy(
+                src_ref=packed.at[0, :, lanes],
+                dst_ref=members.at[rows, lanes],
+                send_sem=patch_send.at[c, k],
+                recv_sem=patch_recv.at[c, source(k)],
+                device_id=(peer(k), tile),
+                device_id_type=MESH,
+            )
+
+        return one
+
+    def back_arrival(c):
+        lanes = pl.ds(piece * c, piece)
+
+        def one(k):
+            return pltpu.make_async_remote_copy(
+                src_ref=result.at[pl.ds(0, own), lanes],
+                dst_ref=back.at[source(k), :, lanes],
+                send_sem=back_send.at[c, k],
+                recv_sem=back_recv.at[c, source(k)],
+                device_id=(peer(k), tile),
+                device_id_type=MESH,
+            )
+
+        return one
+
+    def for_all(make, act):
+        def one(k, carry):
+            act(make(k))
+            return carry
+
+        lax.fori_loop(1, parts, one, 0)
+
+    start = lambda copy: copy.start()
+    wait_send = lambda copy: copy.wait_send()
+    wait_recv = lambda copy: copy.wait_recv()
+
+    for_all(seen_copy, start)
     for role in range(3):
         seen[role, mine, :] = picked[me + role]
     members[mine, :] = packed[me]
-    lax.fori_loop(1, parts, wait_seen, 0)
+    for_all(seen_arrival, wait_recv)
+    for c in range(CHUNKS):
+        for_all(patch_copy(c), start)
 
     row_id = lax.broadcasted_iota(jnp.int32, (size, size), 0)
     column_id = lax.broadcasted_iota(jnp.int32, (size, size), 1)
@@ -355,7 +403,6 @@
             )
         )
     square = jnp.sum(jnp.sum(gram * gram, axis=0, keepdims=True), axis=1, keepdims=True)
-    inverse_scale = lax.rsqrt(square)
     inverse_scale = 1.0 / jnp.sqrt(square)
 
     def put(parts_ref, value):
@@ -394,28 +441,16 @@
     mean_weight = jnp.sum(root[...] * once, axis=0, keepdims=True) * inverse_scale
     put(root_parts, jnp.sqrt((size - 1.0) * inverse_scale) * root[...] + mean_weight)
 
-    lax.fori_loop(1, parts, wait_patch, 0)
-    chunk = 256
-    for c in range(cells // chunk):
-        lanes = pl.ds(chunk * c, chunk)
-        block = members[:, lanes]
-        center = jnp.sum(block, axis=0, keepdims=True) * (1.0 / size)
-        high, low = split(block - center)
-        result[:, lanes] = center + dot3(root_parts[0], root_parts[1], high, low)
-    start_all(back_copy)
-    back[me] = result[mine, :]
-    lax.fori_loop(1, parts, wait_back, 0)
-    for copy in halo:
-        copy.wait_send()
-    wait_send_all(seen_copy)
-    wait_send_all(patch_copy)
-    wait_send_all(back_copy)
-
-
-def unpack_kernel(back, out, rows_ref, sem):
-    own = back.shape[1]
-    lane_tiles = rows_ref.shape[2] // 128
-    group = lax.broadcasted_iota(jnp.int32, (8, 128), 1) // COLS
+    width_at_once = min(piece, 256)
+    for c in range(CHUNKS):
+        for_all(patch_arrival(c), wait_recv)
+        for first in range(piece * c, piece * (c + 1), width_at_once):
+            lanes = pl.ds(first, width_at_once)
+            block = members[:, lanes]
+            center = jnp.sum(block, axis=0, keepdims=True) * (1.0 / size)
+            high, low = split(block - center)
+            result[:, lanes] = center + dot3(root_parts[0], root_parts[1], high, low)
+        for_all(back_copy(c), start)
 
     def unpack(g, carry):
         lanes = pl.ds(pl.multiple_of(g * 128, 128), 128)
@@ -424,17 +459,30 @@
             for block in range(lane_tiles):
                 values = [back[8 * block + p, at, lanes] for p in range(8)]
                 for r, value in enumerate(exchange_groups(values, group)):
-                    rows_ref[8 * g + r, at, pl.ds(128 * block, 128)] = value
+                    levels[0, 8 * g + r, at, pl.ds(128 * block, 128)] = value
         return carry
 
-    lax.fori_loop(0, ROWS // 8, unpack, 0)
-    copies = [
-        pltpu.make_async_copy(rows_ref.at[:, m], out.at[m], sem.at[m]) for m in range(own)
-    ]
-    for copy in copies:
-        copy.start()
-    for copy in copies:
-        copy.wait()
+    back[me] = result[mine, :]
+    for copy in halo:
+        copy.wait_send()
+    stores = []
+    for c in range(CHUNKS):
+        for_all(back_arrival(c), wait_recv)
+        groups = ROWS // 8 // CHUNKS
+        lax.fori_loop(groups * c, groups * (c + 1), unpack, 0)
+        rows = pl.ds(ROWS // CHUNKS * c, ROWS // CHUNKS)
+        for m in range(own):
+            store = pltpu.make_async_copy(
+                levels.at[0, rows, m], out.at[m, rows], out_sem.at[c, m]
+            )
+            store.start()
+            stores.append(store)
+    for_all(seen_copy, wait_send)
+    for c in range(CHUNKS):
+        for_all(patch_copy(c), wait_send)
+        for_all(back_copy(c), wait_send)
+    for store in stores:
+        store.wait()
 
 
 def body(*args, parts, tiles):
@@ -450,11 +498,11 @@
     smem = pl.BlockSpec(memory_space=pltpu.SMEM)
     tall = ROWS + 2 * PAD
     pair = pltpu.VMEM((2, size, size), jnp.bfloat16)
-    back = pl.pallas_call(
+    return pl.pallas_call(
         functools.partial(main_kernel, parts=parts, tiles=tiles),
-        out_shape=jax.ShapeDtypeStruct((parts, own, cells), f32),
+        out_shape=jax.ShapeDtypeStruct(field.shape, f32),
         in_specs=[hbm] * 4 + [vmem] * 4 + [smem],
-        out_specs=vmem,
+        out_specs=hbm,
         scratch_shapes=[
             pltpu.VMEM((PASSES + 1, tall, own, width), f32),
             pltpu.VMEM((3, tall, width), f32),
@@ -463,36 +511,29 @@
             pltpu.VMEM((parts + 2, own, nobs), f32),
             pltpu.VMEM((size, cells), f32),
             pltpu.VMEM((3, size, nobs), f32),
-            pltpu.VMEM((8, 128), f32),
             pltpu.VMEM((size, size), f32),
             pair,
             pair,
             pair,
-            pltpu.VMEM((8, 128), f32),
+            pltpu.VMEM((parts, own, cells), f32),
             pltpu.VMEM((size, cells), f32),
             dma((own + 3,)),
+            dma((CHUNKS, own)),
+            pltpu.SemaphoreType.REGULAR((4,)),
             dma((4,)),
             dma((4,)),
             dma((parts,)),
             dma((parts,)),
-            dma((parts,)),
-            dma((parts,)),
-            dma((parts,)),
-            dma((parts,)),
+            dma((CHUNKS, parts)),
+            dma((CHUNKS, parts)),
+            dma((CHUNKS, parts)),
+            dma((CHUNKS, parts)),
         ],
         compiler_params=pltpu.CompilerParams(
             collective_id=0, has_side_effects=True, vmem_limit_bytes=VMEM_LIMIT
         ),
         name="forecast_and_analysis",
     )(*args)
-    return pl.pallas_call(
-        unpack_kernel,
-        out_shape=jax.ShapeDtypeStruct(field.shape, f32),
-        in_specs=[vmem],
-        out_specs=hbm,
-        scratch_shapes=[pltpu.VMEM((ROWS, own, width), f32), dma((own,))],
-        name="unpack",
-    )(back)
 
 
 def solution(mesh):

time: 123 us -> 95.4 us (0.78)
  the two profiles are of different devices: /device:TPU:1 before, /device:TPU:88 now
where the time goes in v1:
time: 95.4 us; the launch traced here: 94.3 us
  Pallas kernels  91.1 us (95%)
  local copies, waits for them, and re-layouts  3.14 us (3%)
    pallas_call x1, Pallas kernels, body(): pl.pallas_call(functools.partial(main_kernel, parts=parts, tiles=tiles),...  91.1 us
    unnamed x1, local copies, waits for them, and re-layouts  3.14 us

profile of v1, /device:TPU:88, one launch (start us, length us, event | category | flops | bytes accessed | tf_op | source)
XLA Modules:
  0.0 94.3 jit_solution(13651095976689639419)
XLA Ops:
  0.0 91.1 %forecast_and_analysis.1 = f32[16,64,512]{2,1,0:T(8,128)} custom-call(f32[16,64,512]{2,1,0:T(8,128)} %field.1, f32[64,512]{1,0:T(8,128)} %coef_x.1, f32[64,512]{1,0:T(8,128)} %coef_y.1, f32[64,512]{1,0:T(8,128)} %coef_mix.1, f32[1,32,128]{2,1,0:T(8,128)} %obs_value.1, f32[1,32,128]{2,1,0:T(8,128)} %obs_error.1, s32[1,32,128]{2,1,0:T(8,128)} %obs_index.1, ...), custom_call_target="tpu_custom_call" | custom-call | tf_op jit(solution)/shard_map/forecast_and_analysis/pallas_call | solution.py:501
  91.1 3.1 %copy.11 = f32[16,64,512]{2,1,0:T(8,128)} copy(f32[16,64,512]{2,1,0:T(8,128)} %forecast_and_analysis.1) | data formatting | bytes 4194304

commit v2 on v1

--- a/solution.py
+++ b/solution.py
@@ -12,8 +12,10 @@
 PAD = 8
 ROWS = 64
 COLS = 16
-UNROLL = 8
-CHUNKS = 2
+UNROLL = 16
+CHUNKS = 4
+EARLY = 1
+ORDER = (1, 2, 3, 4, 5, 6, 0, 7)
 MESH = pl.DeviceIdType.MESH
 VMEM_LIMIT = 62 * 1024 * 1024
 
@@ -212,8 +214,8 @@
 
     group = lax.broadcasted_iota(jnp.int32, (8, 128), 1) // COLS
 
-    def pack(g, carry):
-        lanes = pl.ds(pl.multiple_of(g * 128, 128), 128)
+    def pack(place, g):
+        lanes = pl.ds(pl.multiple_of(place * 128, 128), 128)
         for half in range(own // 8):
             at = pl.ds(8 * half, 8)
             for block in range(lane_tiles):
@@ -223,14 +225,122 @@
                 ]
                 for p, value in enumerate(exchange_groups(rows, group)):
                     packed[8 * block + p, at, lanes] = value
+
+    def pack_inner(place, carry):
+        pack(place, place + 1)
         return carry
+
+    mine = pl.ds(pl.multiple_of(own * me, own), own)
+
+    def seen_copy(k):
+        return pltpu.make_async_remote_copy(
+            src_ref=picked.at[pl.ds(peer(k), 3)],
+            dst_ref=seen.at[:, mine],
+            send_sem=seen_send.at[k],
+            recv_sem=seen_recv.at[me],
+            device_id=(peer(k), tile),
+            device_id_type=MESH,
+        )
+
+    piece = cells // CHUNKS
+
+    def patch_copy(c):
+        lanes = pl.ds(piece * c, piece)
+
+        def one(k):
+            return pltpu.make_async_remote_copy(
+                src_ref=packed.at[peer(k), :, lanes],
+                dst_ref=members.at[mine, lanes],
+                send_sem=patch_send.at[c, k],
+                recv_sem=patch_recv.at[c, me],
+                device_id=(peer(k), tile),
+                device_id_type=MESH,
+            )
+
+        return one
+
+    def back_copy(c):
+        lanes = pl.ds(piece * c, piece)
+
+        def one(k):
+            rows = pl.ds(pl.multiple_of(own * peer(k), own), own)
+            return pltpu.make_async_remote_copy(
+                src_ref=result.at[rows, lanes],
+                dst_ref=back.at[me, :, lanes],
+                send_sem=back_send.at[c, k],
+                recv_sem=back_recv.at[c, me],
+                device_id=(peer(k), tile),
+                device_id_type=MESH,
+            )
+
+        return one
+
+    def seen_arrival(k):
+        rows = pl.ds(pl.multiple_of(own * source(k), own), own)
+        return pltpu.make_async_remote_copy(
+            src_ref=picked.at[pl.ds(0, 3)],
+            dst_ref=seen.at[:, rows],
+            send_sem=seen_send.at[k],
+            recv_sem=seen_recv.at[source(k)],
+            device_id=(peer(k), tile),
+            device_id_type=MESH,
+        )
+
+    def patch_arrival(c):
+        lanes = pl.ds(piece * c, piece)
+
+        def one(k):
+            rows = pl.ds(pl.multiple_of(own * source(k), own), own)
+            return pltpu.make_async_remote_copy(
+                src_ref=packed.at[0, :, lanes],
+                dst_ref=members.at[rows, lanes],
+                send_sem=patch_send.at[c, k],
+                recv_sem=patch_recv.at[c, source(k)],
+                device_id=(peer(k), tile),
+                device_id_type=MESH,
+            )
+
+        return one
+
+    def back_arrival(c):
+        lanes = pl.ds(piece * c, piece)
+
+        def one(k):
+            return pltpu.make_async_remote_copy(
+                src_ref=result.at[pl.ds(0, own), lanes],
+                dst_ref=back.at[source(k), :, lanes],
+                send_sem=back_send.at[c, k],
+                recv_sem=back_recv.at[c, source(k)],
+                device_id=(peer(k), tile),
+                device_id_type=MESH,
+            )
+
+        return one
+
+    def for_all(make, act):
+        def one(k, carry):
+            act(make(k))
+            return carry
+
+        lax.fori_loop(1, parts, one, 0)
+
+    start = lambda copy: copy.start()
+    wait_send = lambda copy: copy.wait_send()
+    wait_recv = lambda copy: copy.wait_recv()
 
     lax.fori_loop(PAD, PAD + ROWS, widen, 0, unroll=4)
     news = spread_news()
     for k in range(1, PASSES + 1):
         step(k - 1, PAD + k, ROWS - 2 * k)
         next(news, None)
-    lax.fori_loop(1, ROWS // 8 - 1, pack, 0)
+    for _ in news:
+        pass
+    per_chunk = ROWS // 8 // CHUNKS
+    inner = ROWS // 8 - 2
+    lax.fori_loop(0, per_chunk * EARLY, pack_inner, 0)
+    for c in range(EARLY):
+        for_all(patch_copy(c), start)
+    lax.fori_loop(per_chunk * EARLY, inner, pack_inner, 0)
     for copy in halo:
         copy.wait_recv()
     lax.fori_loop(PAD - PASSES, PAD, widen, 0, unroll=6)
@@ -239,10 +349,8 @@
         for i in range(PASSES):
             advance(k - 1, PAD - PASSES + k + i)
             advance(k - 1, PAD + ROWS - k + i)
-    pack(0, 0)
-    pack(ROWS // 8 - 1, 0)
-    for _ in news:
-        pass
+    for place in range(inner, ROWS // 8):
+        pack(place, ORDER[place])
 
     def pick(b, carry):
         index = jnp.broadcast_to(obs_index[0, pl.ds(b, 1), :], (8, nobs))
@@ -255,118 +363,20 @@
                 found = jnp.take_along_axis(
                     packed[b, at, pl.ds(128 * g, 128)], lane, axis=1, mode="promise_in_bounds"
                 )
-                total = jnp.where(place == g, found, total)
+                total = jnp.where(place == ORDER[g], found, total)
             picked[b + 1, at, :] = total
         return carry
 
     lax.fori_loop(0, parts, pick, 0, unroll=4)
     picked[0] = picked[parts]
     picked[parts + 1] = picked[1]
-
-    mine = pl.ds(pl.multiple_of(own * me, own), own)
-
-    def seen_copy(k):
-        return pltpu.make_async_remote_copy(
-            src_ref=picked.at[pl.ds(peer(k), 3)],
-            dst_ref=seen.at[:, mine],
-            send_sem=seen_send.at[k],
-            recv_sem=seen_recv.at[me],
-            device_id=(peer(k), tile),
-            device_id_type=MESH,
-        )
-
-    piece = cells // CHUNKS
-
-    def patch_copy(c):
-        lanes = pl.ds(piece * c, piece)
-
-        def one(k):
-            return pltpu.make_async_remote_copy(
-                src_ref=packed.at[peer(k), :, lanes],
-                dst_ref=members.at[mine, lanes],
-                send_sem=patch_send.at[c, k],
-                recv_sem=patch_recv.at[c, me],
-                device_id=(peer(k), tile),
-                device_id_type=MESH,
-            )
-
-        return one
-
-    def back_copy(c):
-        lanes = pl.ds(piece * c, piece)
-
-        def one(k):
-            rows = pl.ds(pl.multiple_of(own * peer(k), own), own)
-            return pltpu.make_async_remote_copy(
-                src_ref=result.at[rows, lanes],
-                dst_ref=back.at[me, :, lanes],
-                send_sem=back_send.at[c, k],
-                recv_sem=back_recv.at[c, me],
-                device_id=(peer(k), tile),
-                device_id_type=MESH,
-            )
-
-        return one
-
-    def seen_arrival(k):
-        rows = pl.ds(pl.multiple_of(own * source(k), own), own)
-        return pltpu.make_async_remote_copy(
-            src_ref=picked.at[pl.ds(0, 3)],
-            dst_ref=seen.at[:, rows],
-            send_sem=seen_send.at[k],
-            recv_sem=seen_recv.at[source(k)],
-            device_id=(peer(k), tile),
-            device_id_type=MESH,
-        )
-
-    def patch_arrival(c):
-        lanes = pl.ds(piece * c, piece)
-
-        def one(k):
-            rows = pl.ds(pl.multiple_of(own * source(k), own), own)
-            return pltpu.make_async_remote_copy(
-                src_ref=packed.at[0, :, lanes],
-                dst_ref=members.at[rows, lanes],
-                send_sem=patch_send.at[c, k],
-                recv_sem=patch_recv.at[c, source(k)],
-                device_id=(peer(k), tile),
-                device_id_type=MESH,
-            )
-
-        return one
-
-    def back_arrival(c):
-        lanes = pl.ds(piece * c, piece)
-
-        def one(k):
-            return pltpu.make_async_remote_copy(
-                src_ref=result.at[pl.ds(0, own), lanes],
-                dst_ref=back.at[source(k), :, lanes],
-                send_sem=back_send.at[c, k],
-                recv_sem=back_recv.at[c, source(k)],
-                device_id=(peer(k), tile),
-                device_id_type=MESH,
-            )
-
-        return one
-
-    def for_all(make, act):
-        def one(k, carry):
-            act(make(k))
-            return carry
-
-        lax.fori_loop(1, parts, one, 0)
-
-    start = lambda copy: copy.start()
-    wait_send = lambda copy: copy.wait_send()
-    wait_recv = lambda copy: copy.wait_recv()
 
     for_all(seen_copy, start)
     for role in range(3):
         seen[role, mine, :] = picked[me + role]
     members[mine, :] = packed[me]
     for_all(seen_arrival, wait_recv)
-    for c in range(CHUNKS):
+    for c in range(EARLY, CHUNKS):
         for_all(patch_copy(c), start)
 
     row_id = lax.broadcasted_iota(jnp.int32, (size, size), 0)
@@ -452,15 +462,14 @@
             result[:, lanes] = center + dot3(root_parts[0], root_parts[1], high, low)
         for_all(back_copy(c), start)
 
-    def unpack(g, carry):
-        lanes = pl.ds(pl.multiple_of(g * 128, 128), 128)
+    def unpack(place, g):
+        lanes = pl.ds(128 * place, 128)
         for half in range(own // 8):
             at = pl.ds(8 * half, 8)
             for block in range(lane_tiles):
                 values = [back[8 * block + p, at, lanes] for p in range(8)]
                 for r, value in enumerate(exchange_groups(values, group)):
                     levels[0, 8 * g + r, at, pl.ds(128 * block, 128)] = value
-        return carry
 
     back[me] = result[mine, :]
     for copy in halo:
@@ -468,15 +477,16 @@
     stores = []
     for c in range(CHUNKS):
         for_all(back_arrival(c), wait_recv)
-        groups = ROWS // 8 // CHUNKS
-        lax.fori_loop(groups * c, groups * (c + 1), unpack, 0)
-        rows = pl.ds(ROWS // CHUNKS * c, ROWS // CHUNKS)
-        for m in range(own):
-            store = pltpu.make_async_copy(
-                levels.at[0, rows, m], out.at[m, rows], out_sem.at[c, m]
-            )
-            store.start()
-            stores.append(store)
+        for place in range(per_chunk * c, per_chunk * (c + 1)):
+            g = ORDER[place]
+            unpack(place, g)
+            rows = pl.ds(8 * g, 8)
+            for m in range(own):
+                store = pltpu.make_async_copy(
+                    levels.at[0, rows, m], out.at[m, rows], out_sem.at[g, m]
+                )
+                store.start()
+                stores.append(store)
     for_all(seen_copy, wait_send)
     for c in range(CHUNKS):
         for_all(patch_copy(c), wait_send)
@@ -518,7 +528,7 @@
             pltpu.VMEM((parts, own, cells), f32),
             pltpu.VMEM((size, cells), f32),
             dma((own + 3,)),
-            dma((CHUNKS, own)),
+            dma((ROWS // 8, own)),
             pltpu.SemaphoreType.REGULAR((4,)),
             dma((4,)),
             dma((4,)),

time: 95.4 us -> 99.9 us (1.047)
  Pallas kernels: 91.1 us -> 95.2 us
    pallas_call x1, Pallas kernels: 91.1 us -> 95.2 us  [body(): pl.pallas_call(functools.partial(main_kernel, parts=parts, tiles=tiles),...]
where the time goes in v2:
time: 99.9 us; the launch traced here: 98.3 us
  Pallas kernels  95.2 us (95%)
  local copies, waits for them, and re-layouts  3.14 us (3%)
    pallas_call x1, Pallas kernels, body(): pl.pallas_call(functools.partial(main_kernel, parts=parts, tiles=tiles),...  95.2 us
    unnamed x1, local copies, waits for them, and re-layouts  3.14 us

profile of v2, /device:TPU:88, one launch (start us, length us, event | category | flops | bytes accessed | tf_op | source)
XLA Modules:
  0.0 98.3 jit_solution(13351913672550827563)
XLA Ops:
  0.0 95.2 %forecast_and_analysis.1 = f32[16,64,512]{2,1,0:T(8,128)} custom-call(f32[16,64,512]{2,1,0:T(8,128)} %field.1, f32[64,512]{1,0:T(8,128)} %coef_x.1, f32[64,512]{1,0:T(8,128)} %coef_y.1, f32[64,512]{1,0:T(8,128)} %coef_mix.1, f32[1,32,128]{2,1,0:T(8,128)} %obs_value.1, f32[1,32,128]{2,1,0:T(8,128)} %obs_error.1, s32[1,32,128]{2,1,0:T(8,128)} %obs_index.1, ...), custom_call_target="tpu_custom_call" | custom-call | tf_op jit(solution)/shard_map/forecast_and_analysis/pallas_call | solution.py:511
  95.2 3.1 %copy.11 = f32[16,64,512]{2,1,0:T(8,128)} copy(f32[16,64,512]{2,1,0:T(8,128)} %forecast_and_analysis.1) | data formatting | bytes 4194304

commit v3 on v2

--- a/solution.py
+++ b/solution.py
@@ -13,7 +13,7 @@
 ROWS = 64
 COLS = 16
 UNROLL = 16
-CHUNKS = 4
+PIECES = ((0, 2), (2, 5), (5, 8))
 EARLY = 1
 ORDER = (1, 2, 3, 4, 5, 6, 0, 7)
 MESH = pl.DeviceIdType.MESH
@@ -101,9 +101,6 @@
     def peer(k):
         return lax.rem(me + 11 * k, parts)
 
-    def source(k):
-        return lax.rem(me + 12 * parts - 11 * k, parts)
-
     loads = []
     for m in range(own):
         loads.append(
@@ -236,23 +233,25 @@
         return pltpu.make_async_remote_copy(
             src_ref=picked.at[pl.ds(peer(k), 3)],
             dst_ref=seen.at[:, mine],
-            send_sem=seen_send.at[k],
-            recv_sem=seen_recv.at[me],
+            send_sem=seen_send,
+            recv_sem=seen_recv,
             device_id=(peer(k), tile),
             device_id_type=MESH,
         )
 
-    piece = cells // CHUNKS
+    others = parts - 1
+
+    def lanes_of(c):
+        first, last = PIECES[c]
+        return pl.ds(128 * first, 128 * (last - first))
 
     def patch_copy(c):
-        lanes = pl.ds(piece * c, piece)
-
         def one(k):
             return pltpu.make_async_remote_copy(
-                src_ref=packed.at[peer(k), :, lanes],
-                dst_ref=members.at[mine, lanes],
-                send_sem=patch_send.at[c, k],
-                recv_sem=patch_recv.at[c, me],
+                src_ref=packed.at[peer(k), :, lanes_of(c)],
+                dst_ref=members.at[mine, lanes_of(c)],
+                send_sem=patch_send,
+                recv_sem=patch_recv.at[c],
                 device_id=(peer(k), tile),
                 device_id_type=MESH,
             )
@@ -260,73 +259,52 @@
         return one
 
     def back_copy(c):
-        lanes = pl.ds(piece * c, piece)
-
         def one(k):
             rows = pl.ds(pl.multiple_of(own * peer(k), own), own)
             return pltpu.make_async_remote_copy(
-                src_ref=result.at[rows, lanes],
-                dst_ref=back.at[me, :, lanes],
-                send_sem=back_send.at[c, k],
-                recv_sem=back_recv.at[c, me],
+                src_ref=result.at[rows, lanes_of(c)],
+                dst_ref=back.at[me, :, lanes_of(c)],
+                send_sem=back_send,
+                recv_sem=back_recv.at[c],
                 device_id=(peer(k), tile),
                 device_id_type=MESH,
             )
 
         return one
 
-    def seen_arrival(k):
-        rows = pl.ds(pl.multiple_of(own * source(k), own), own)
+    def start_all(make):
+        def one(k, carry):
+            make(k).start()
+            return carry
+
+        lax.fori_loop(1, parts, one, 0)
+
+    def together(src, dst, send_sem, recv_sem):
         return pltpu.make_async_remote_copy(
-            src_ref=picked.at[pl.ds(0, 3)],
-            dst_ref=seen.at[:, rows],
-            send_sem=seen_send.at[k],
-            recv_sem=seen_recv.at[source(k)],
-            device_id=(peer(k), tile),
+            src_ref=src,
+            dst_ref=dst,
+            send_sem=send_sem,
+            recv_sem=recv_sem,
+            device_id=(peer(1), tile),
             device_id_type=MESH,
         )
 
-    def patch_arrival(c):
-        lanes = pl.ds(piece * c, piece)
-
-        def one(k):
-            rows = pl.ds(pl.multiple_of(own * source(k), own), own)
-            return pltpu.make_async_remote_copy(
-                src_ref=packed.at[0, :, lanes],
-                dst_ref=members.at[rows, lanes],
-                send_sem=patch_send.at[c, k],
-                recv_sem=patch_recv.at[c, source(k)],
-                device_id=(peer(k), tile),
-                device_id_type=MESH,
-            )
-
-        return one
-
-    def back_arrival(c):
-        lanes = pl.ds(piece * c, piece)
-
-        def one(k):
-            return pltpu.make_async_remote_copy(
-                src_ref=result.at[pl.ds(0, own), lanes],
-                dst_ref=back.at[source(k), :, lanes],
-                send_sem=back_send.at[c, k],
-                recv_sem=back_recv.at[c, source(k)],
-                device_id=(peer(k), tile),
-                device_id_type=MESH,
-            )
-
-        return one
-
-    def for_all(make, act):
-        def one(k, carry):
-            act(make(k))
-            return carry
-
-        lax.fori_loop(1, parts, one, 0)
-
-    start = lambda copy: copy.start()
-    wait_send = lambda copy: copy.wait_send()
-    wait_recv = lambda copy: copy.wait_recv()
+    most = pl.ds(0, own * others)
+    seen_all = together(
+        seen.at[:, most], seen.at[:, most], seen_send, seen_recv
+    )
+
+    def patch_all(c):
+        return together(
+            result.at[most, lanes_of(c)], members.at[most, lanes_of(c)], patch_send, patch_recv.at[c]
+        )
+
+    def back_all(c):
+        src, dst = packed.at[pl.ds(0, others), :, lanes_of(c)], back.at[pl.ds(0, others), :, lanes_of(c)]
+        return together(src, dst, back_send, back_recv.at[c])
+
+    patch_sent = together(members.at[most], result.at[most], patch_send, patch_recv.at[0])
+    back_sent = together(members.at[most], result.at[most], back_send, back_recv.at[0])
 
     lax.fori_loop(PAD, PAD + ROWS, widen, 0, unroll=4)
     news = spread_news()
@@ -335,12 +313,13 @@
         next(news, None)
     for _ in news:
         pass
-    per_chunk = ROWS // 8 // CHUNKS
     inner = ROWS // 8 - 2
-    lax.fori_loop(0, per_chunk * EARLY, pack_inner, 0)
+    packed_early = PIECES[EARLY][0]
+    if packed_early:
+        lax.fori_loop(0, packed_early, pack_inner, 0)
     for c in range(EARLY):
-        for_all(patch_copy(c), start)
-    lax.fori_loop(per_chunk * EARLY, inner, pack_inner, 0)
+        start_all(patch_copy(c))
+    lax.fori_loop(packed_early, inner, pack_inner, 0)
     for copy in halo:
         copy.wait_recv()
     lax.fori_loop(PAD - PASSES, PAD, widen, 0, unroll=6)
@@ -371,13 +350,13 @@
     picked[0] = picked[parts]
     picked[parts + 1] = picked[1]
 
-    for_all(seen_copy, start)
+    start_all(seen_copy)
     for role in range(3):
         seen[role, mine, :] = picked[me + role]
     members[mine, :] = packed[me]
-    for_all(seen_arrival, wait_recv)
-    for c in range(EARLY, CHUNKS):
-        for_all(patch_copy(c), start)
+    seen_all.wait_recv()
+    for c in range(EARLY, len(PIECES)):
+        start_all(patch_copy(c))
 
     row_id = lax.broadcasted_iota(jnp.int32, (size, size), 0)
     column_id = lax.broadcasted_iota(jnp.int32, (size, size), 1)
@@ -451,16 +430,16 @@
     mean_weight = jnp.sum(root[...] * once, axis=0, keepdims=True) * inverse_scale
     put(root_parts, jnp.sqrt((size - 1.0) * inverse_scale) * root[...] + mean_weight)
 
-    width_at_once = min(piece, 256)
-    for c in range(CHUNKS):
-        for_all(patch_arrival(c), wait_recv)
-        for first in range(piece * c, piece * (c + 1), width_at_once):
-            lanes = pl.ds(first, width_at_once)
+    for c, (first_block, last_block) in enumerate(PIECES):
+        patch_all(c).wait_recv()
+        for first in range(first_block, last_block, 2):
+            many = min(2, last_block - first)
+            lanes = pl.ds(128 * first, 128 * many)
             block = members[:, lanes]
             center = jnp.sum(block, axis=0, keepdims=True) * (1.0 / size)
             high, low = split(block - center)
             result[:, lanes] = center + dot3(root_parts[0], root_parts[1], high, low)
-        for_all(back_copy(c), start)
+        start_all(back_copy(c))
 
     def unpack(place, g):
         lanes = pl.ds(128 * place, 128)
@@ -475,9 +454,9 @@
     for copy in halo:
         copy.wait_send()
     stores = []
-    for c in range(CHUNKS):
-        for_all(back_arrival(c), wait_recv)
-        for place in range(per_chunk * c, per_chunk * (c + 1)):
+    for c, (first_block, last_block) in enumerate(PIECES):
+        back_all(c).wait_recv()
+        for place in range(first_block, last_block):
             g = ORDER[place]
             unpack(place, g)
             rows = pl.ds(8 * g, 8)
@@ -487,10 +466,9 @@
                 )
                 store.start()
                 stores.append(store)
-    for_all(seen_copy, wait_send)
-    for c in range(CHUNKS):
-        for_all(patch_copy(c), wait_send)
-        for_all(back_copy(c), wait_send)
+    seen_all.wait_send()
+    patch_sent.wait_send()
+    back_sent.wait_send()
     for store in stores:
         store.wait()
 
@@ -532,12 +510,12 @@
             pltpu.SemaphoreType.REGULAR((4,)),
             dma((4,)),
             dma((4,)),
-            dma((parts,)),
-            dma((parts,)),
-            dma((CHUNKS, parts)),
-            dma((CHUNKS, parts)),
-            dma((CHUNKS, parts)),
-            dma((CHUNKS, parts)),
+            dma,
+            dma,
+            dma,
+            dma((len(PIECES),)),
+            dma,
+            dma((len(PIECES),)),
         ],
         compiler_params=pltpu.CompilerParams(
             collective_id=0, has_side_effects=True, vmem_limit_bytes=VMEM_LIMIT

time: 99.9 us -> 92.2 us (0.923); the launches traced: 98.3 us -> 92 us
  Pallas kernels: 95.2 us -> 88.8 us
    pallas_call x1, Pallas kernels: 95.2 us -> 88.8 us  [body(): pl.pallas_call(functools.partial(main_kernel, parts=parts, tiles=tiles),...]
where the time goes in v3:
time: 92.2 us; the launch traced here: 92 us
  Pallas kernels  88.8 us (96%)
  local copies, waits for them, and re-layouts  3.14 us (3%)
    pallas_call x1, Pallas kernels, body(): pl.pallas_call(functools.partial(main_kernel, parts=parts, tiles=tiles),...  88.8 us
    unnamed x1, local copies, waits for them, and re-layouts  3.14 us

profile of v3, /device:TPU:88, one launch (start us, length us, event | category | flops | bytes accessed | tf_op | source)
XLA Modules:
  0.0 92.0 jit_solution(9562890763441025262)
XLA Ops:
  0.0 88.8 %forecast_and_analysis.1 = f32[16,64,512]{2,1,0:T(8,128)} custom-call(f32[16,64,512]{2,1,0:T(8,128)} %field.1, f32[64,512]{1,0:T(8,128)} %coef_x.1, f32[64,512]{1,0:T(8,128)} %coef_y.1, f32[64,512]{1,0:T(8,128)} %coef_mix.1, f32[1,32,128]{2,1,0:T(8,128)} %obs_value.1, f32[1,32,128]{2,1,0:T(8,128)} %obs_error.1, s32[1,32,128]{2,1,0:T(8,128)} %obs_index.1, ...), custom_call_target="tpu_custom_call" | custom-call | tf_op jit(solution)/shard_map/forecast_and_analysis/pallas_call | solution.py:489
  88.8 3.1 %copy.11 = f32[16,64,512]{2,1,0:T(8,128)} copy(f32[16,64,512]{2,1,0:T(8,128)} %forecast_and_analysis.1) | data formatting | bytes 4194304

commit v4 on v3

--- a/solution.py
+++ b/solution.py
@@ -316,10 +316,10 @@
     inner = ROWS // 8 - 2
     packed_early = PIECES[EARLY][0]
     if packed_early:
-        lax.fori_loop(0, packed_early, pack_inner, 0)
+        lax.fori_loop(0, packed_early, pack_inner, 0, unroll=2)
     for c in range(EARLY):
         start_all(patch_copy(c))
-    lax.fori_loop(packed_early, inner, pack_inner, 0)
+    lax.fori_loop(packed_early, inner, pack_inner, 0, unroll=2)
     for copy in halo:
         copy.wait_recv()
     lax.fori_loop(PAD - PASSES, PAD, widen, 0, unroll=6)
@@ -346,7 +346,7 @@
             picked[b + 1, at, :] = total
         return carry
 
-    lax.fori_loop(0, parts, pick, 0, unroll=4)
+    lax.fori_loop(0, parts, pick, 0, unroll=8)
     picked[0] = picked[parts]
     picked[parts + 1] = picked[1]
 

time: 92.2 us -> 94.7 us (1.027)
  Pallas kernels: 88.8 us -> 91.1 us
    pallas_call x1, Pallas kernels: 88.8 us -> 91.1 us  [body(): pl.pallas_call(functools.partial(main_kernel, parts=parts, tiles=tiles),...]
where the time goes in v4:
time: 94.7 us; the launch traced here: 94.2 us
  Pallas kernels  91.1 us (96%)
  local copies, waits for them, and re-layouts  3.14 us (3%)
    pallas_call x1, Pallas kernels, body(): pl.pallas_call(functools.partial(main_kernel, parts=parts, tiles=tiles),...  91.1 us
    unnamed x1, local copies, waits for them, and re-layouts  3.14 us

profile of v4, /device:TPU:88, one launch (start us, length us, event | category | flops | bytes accessed | tf_op | source)
XLA Modules:
  0.0 94.2 jit_solution(6269439618071848633)
XLA Ops:
  0.0 91.1 %forecast_and_analysis.1 = f32[16,64,512]{2,1,0:T(8,128)} custom-call(f32[16,64,512]{2,1,0:T(8,128)} %field.1, f32[64,512]{1,0:T(8,128)} %coef_x.1, f32[64,512]{1,0:T(8,128)} %coef_y.1, f32[64,512]{1,0:T(8,128)} %coef_mix.1, f32[1,32,128]{2,1,0:T(8,128)} %obs_value.1, f32[1,32,128]{2,1,0:T(8,128)} %obs_error.1, s32[1,32,128]{2,1,0:T(8,128)} %obs_index.1, ...), custom_call_target="tpu_custom_call" | custom-call | tf_op jit(solution)/shard_map/forecast_and_analysis/pallas_call | solution.py:489
  91.1 3.1 %copy.11 = f32[16,64,512]{2,1,0:T(8,128)} copy(f32[16,64,512]{2,1,0:T(8,128)} %forecast_and_analysis.1) | data formatting | bytes 4194304
